TPU v7x, 256 devices: a 8x8x2 block of a 8x8x16 slice. The times are simulated.
256 devices in a mesh: groups: 2 (over z), rows: 64 (over y, x), cols: 2 (over core).
Axes of the slice: x: 8, y: 8, z: 2, core: 2. Of those that a mesh axis runs over, the one named last changes fastest.
The devices are a block of a 8x8x16 slice.
Arguments:
- feature_table: float32 [262144, 1024], P(('groups', 'rows'), 'cols'), parts along dimension 0, may hold values from -6 to 6
- own_features: float32 [4096, 1024], P(('groups', 'rows'), 'cols'), parts along dimension 0, may hold values from -6 to 6
- neighbor_ids: int32 [4096, 50], P(('groups', 'rows')), parts along dimension 0, may hold values from 0 to 131071, as said below
- importance: float32 [4096, 50], P(('groups', 'rows')), parts along dimension 0, may hold values from 0.5 to 5
- w_self: bfloat16 [1024, 1024], P('cols'), may hold values from -0.1875 to 0.1875
- w_pool: bfloat16 [1024, 1024], P('cols'), may hold values from -0.1875 to 0.1875
- bias: float32 [1024], replicated, may hold values from -6 to 6
Outputs:
- embeddings: float32 [4096, 1024], P(('groups', 'rows'), 'cols'), parts along dimension 0
There are 2 independent parts, one for each index of `groups`. A program takes and returns all parts, laid end to end along the dimension named above; an argument that names none is the same for every part. Nothing has to cross between parts.
Inputs may be any that keep to these rules, and one draw needn't show every extreme that they name: `neighbor_ids`: ids of sampled neighbors in the group's table, repeats allowed. In each aligned block of 16 targets, at most 20 ids fall in any one range [k * 2048, (k + 1) * 2048), and one such range holds exactly 20.
All inputs are finite; a program needn't handle non-finite values.
Results may differ from a plain program's by a relative error of at most 0.0017.
Values may be sent and summed in bfloat16 or wider, within the bound.
A program may use at most 64 MiB of HBM per device.

v0:
```python
from functools import partial

import jax
import jax.numpy as jnp
from jax import lax
from jax.sharding import PartitionSpec as P

NEIGH = 50
TGT_DEV = 16


def from_everyone(array, axis):
    count = lax.axis_size(axis)
    return lax.all_to_all(
        jnp.broadcast_to(array[None], (count, *array.shape)), axis, 0, 0, tiled=True
    )


def over_copies(array, axis):
    everything = from_everyone(array, axis)
    return jnp.sum(everything, axis=0)


def request_slots(id_block, share_block, owners, capacity, rows_dev):
    targets = id_block.shape[0]
    neighbors = id_block.shape[1]
    flat_ids = id_block.reshape(-1)
    owner_of = flat_ids // rows_dev
    local_row = flat_ids - owner_of * rows_dev
    target_of = jnp.arange(targets * neighbors, dtype=jnp.int32) // neighbors
    onehot = (owner_of[:, None] == jnp.arange(owners, dtype=jnp.int32)[None, :]).astype(jnp.int32)
    slot_rank = jnp.sum((jnp.cumsum(onehot, axis=0) - onehot) * onehot, axis=1)
    sending = jnp.zeros((owners, capacity), jnp.int32).at[owner_of, slot_rank].set(local_row)
    packed = (
        jnp.zeros((owners, capacity), jnp.int32)
        .at[owner_of, slot_rank]
        .set(local_row * targets + target_of)
    )
    slot_weight = (
        jnp.zeros((owners, capacity), jnp.float32)
        .at[owner_of, slot_rank]
        .set(share_block.reshape(-1))
    )
    return (owner_of, slot_rank, sending, packed, slot_weight)


def plan_requests(id_rows, shares, blocks, owners, capacity, rows_dev):
    targets = id_rows.shape[0] // blocks
    neighbors = id_rows.shape[1]
    per_block = targets * neighbors
    owner_of, slot_rank, sending, packed, slot_weight = jax.vmap(
        partial(request_slots, owners=owners, capacity=capacity, rows_dev=rows_dev)
    )(id_rows.reshape(blocks, targets, neighbors), shares.reshape(blocks, targets, neighbors))
    block_of = jnp.arange(blocks, dtype=jnp.int32)[:, None]
    column = owner_of * (blocks * capacity) + block_of * capacity + slot_rank
    row_index = block_of * targets + jnp.arange(per_block, dtype=jnp.int32)[None, :] // neighbors
    pool_matrix = (
        jnp.zeros((blocks * targets, owners * blocks * capacity), jnp.float32)
        .at[row_index.reshape(-1), column.reshape(-1)]
        .add(shares.reshape(-1))
    )
    outgoing = jnp.transpose(sending, (1, 0, 2)).reshape(owners, blocks * capacity)
    packed_out = jnp.transpose(packed, (1, 0, 2)).reshape(owners, blocks * capacity)
    weight_out = jnp.transpose(slot_weight, (1, 0, 2)).reshape(owners, blocks * capacity)
    return (pool_matrix, outgoing, packed_out, weight_out)


def finish_rows(preact):
    hidden = jnp.maximum(preact, 0.0)
    return hidden * lax.rsqrt(jnp.mean(hidden * hidden, axis=1, keepdims=True) + 1e-06)


def body(feature_table, own_features, neighbor_ids, importance, w_self, w_pool, bias):
    rows_dev, width_half = feature_table.shape
    owners = lax.axis_size("rows")
    col_count = lax.axis_size("cols")
    capacity = TGT_DEV * NEIGH * 8 // (5 * owners)
    shares = importance / jnp.sum(importance, axis=1, keepdims=True)
    own_round = own_features.astype(jnp.bfloat16)
    pool_matrix, outgoing, packed_out, weight_out = plan_requests(
        neighbor_ids, shares, col_count, owners, capacity, rows_dev
    )
    found = jnp.take(
        feature_table,
        lax.all_to_all(outgoing, "rows", split_axis=0, concat_axis=0, tiled=True),
        axis=0,
    )
    arrived = lax.all_to_all(
        found.astype(jnp.bfloat16), "rows", split_axis=0, concat_axis=0, tiled=True
    ).astype(found.dtype)
    pooled = jnp.dot(
        pool_matrix,
        arrived.reshape(-1, width_half),
        precision=lax.Precision.HIGHEST,
        preferred_element_type=jnp.float32,
    )
    partial_sums = jnp.dot(own_round, w_self, preferred_element_type=jnp.float32) + jnp.dot(
        pooled.astype(jnp.bfloat16), w_pool, preferred_element_type=jnp.float32
    )
    column_start = lax.axis_index("cols") * width_half
    preact = over_copies(partial_sums, "cols") + bias
    embedded = finish_rows(preact)
    return lax.dynamic_slice_in_dim(embedded, column_start, width_half, 1)


def solution(mesh):
    placed = (
        P(("groups", "rows"), "cols"),
        P(("groups", "rows"), "cols"),
        P(("groups", "rows"), None),
        P(("groups", "rows"), None),
        P("cols", None),
        P("cols", None),
        P(),
    )
    return jax.shard_map(
        body, mesh=mesh, in_specs=placed, out_specs=P(("groups", "rows"), "cols"), check_vma=False
    )
```

profile of v0, /device:TPU:513, one launch (start us, length us, event | category | flops | bytes accessed | tf_op | source)
XLA Modules:
  0.0 141.3 jit_solution(16610279856507255810)
XLA Ops:
  0.0 0.0 copy-start
  0.0 0.0 copy-start.6
  0.0 0.0 copy-start.9
  0.0 0.9 reshape_reshape.8
  0.9 0.8 reshape_reshape.9
  1.8 0.1 iota_compare_fusion
  1.9 4.2 %reduce-window.6 = s32[2,64,7,128]{3,1,2,0:T(8,128)S(1)} reduce-window(s32[2,64,7,128]{3,1,2,0:T(8,128)S(1)} %copy_bitcast_fusion, s32[]{:T(128)} %constant.33.clone.1), window={size=1x1x1x128 pad=0_0x0_0x0_0x127_0}, to_apply=%region_0.0 | reduce-window | flops 14565376 | bytes 917508 | tf_op jit(solution)/shard_map/reduce-window
  6.1 0.2 slice.14
  6.2 0.2 copy.22
  6.5 0.2 bitcast_bitcast_fusion
  6.7 0.1 fusion.1
  6.8 0.0 copy-done.6
  6.8 0.1 multiply_reduce_fusion.1
  6.9 0.0 copy-done.9
  6.9 0.1 and_reduce_fusion
  7.0 0.1 reshape.363
  7.1 0.1 reshape.365
  7.2 8.8 %scatter_custom_fusion.1 = s32[2560]{0:T(1024)S(1)} fusion(s32[1600]{0:T(1024)S(1)} %reshape.363, s32[1600]{0:T(1024)S(1)} %reshape.365, s32[]{:T(128)} %constant.33.clone.1), kind=kCustom, calls=%fused_computation.55 | custom fusion | bytes 10244
  16.0 0.1 reshape.346
  16.1 0.1 copy.26
  16.2 31.5 %all_to_all.25 = s32[64,1,40]{2,1,0:T(1,128)S(1)} all-to-all(s32[64,1,40]{2,1,0:T(1,128)S(1)} %copy.26), channel_id=1, replica_groups=mesh['groups'=2,'rows'=64,'cols'=2] {'rows'}, dimensions={0} | all-to-all | bytes 20480 | tf_op jit(solution)/shard_map/all_to_all | solution.py:85
  47.7 0.1 reshape.351
  47.8 10.5 %gather_fusion = bf16[2560,512]{1,0:T(8,128)(2,1)} fusion(f32[2048,512]{1,0:T(8,128)} %param.7, s32[3072]{0:T(1024)S(1)} %pad_clamp_fusion), kind=kCustom, calls=%fused_computation | custom fusion | bytes 5253120 | tf_op jit(solution)/shard_map/jit(_take)/gather | solution.py:83
  58.4 3.2 %select_convert_fusion = bf16[64,40,512]{2,1,0:T(8,128)(2,1)} fusion(bf16[64,40,512]{2,1,0:T(8,128)(2,1)} %bitcast.31, pred[64,40]{1,0:T(8,128)(4,1)S(1)} %compare_and_fusion), kind=kLoop, calls=%fused_computation.3 | loop fusion | flops 1310720 | bytes 5245440 | tf_op jit(solution)/shard_map/convert_element_type | solution.py:89
  61.5 0.0 copy-start.2
  61.6 0.0 copy-start.4
  61.6 0.0 copy-start.8
  61.6 0.0 copy-start.7
  61.6 0.0 copy-start.3
  61.6 7.4 %all-to-all-start.1 = ((bf16[64,40,512]{2,1,0:T(8,128)(2,1)}), bf16[64,40,512]{2,1,0:T(8,128)(2,1)}, u32[]{:S(2)}, u32[]{:S(2)}) async-start(bf16[64,40,512]{2,1,0:T(8,128)(2,1)} %select_convert_fusion), calls=%async_computation.1 | async-start | bytes 5242880 | tf_op jit(solution)/shard_map/all_to_all | solution.py:88
  68.9 0.1 reduce_sum.41
  69.0 0.0 copy-done.2
  69.0 0.1 reshape_reshape.7
  69.2 0.1 broadcast_add_fusion
  69.2 0.1 add.181
  69.3 0.1 add.184
  69.4 0.1 add.185
  69.5 0.0 copy-done.4
  69.5 0.1 reduce_sum.42
  69.6 0.1 broadcast_divide_fusion
  69.7 0.1 reshape.359
  69.8 0.1 compare_select_fusion.2
  69.9 0.0 copy-done.8
  69.9 0.1 multiply_reduce_fusion.2
  70.0 0.0 copy-done.7
  70.0 0.1 and_reduce_fusion.1
  70.1 0.0 copy-start.1
  70.1 10.1 %scatter_custom_fusion = f32[81920]{0:T(1024)S(1)} fusion(s32[1600]{0:T(1024)S(1)} %broadcast_select_fusion, f32[1600]{0:T(1024)S(1)} %reshape.359, f32[]{:T(128)} %constant.24.clone.1), kind=kCustom, calls=%fused_computation.15 | custom fusion | flops 1600 | bytes 327684
  80.2 0.1 reshape.343
  80.3 0.0 copy-done
  80.3 0.0 copy-done.3
  80.3 0.3 fusion.4
  80.6 43.1 %all-to-all-done.1 = bf16[64,40,512]{2,1,0:T(8,128)(2,1)} async-done(((bf16[64,40,512]{2,1,0:T(8,128)(2,1)}), bf16[64,40,512]{2,1,0:T(8,128)(2,1)}, u32[]{:S(2)}, u32[]{:S(2)}) %all-to-all-start.1) | async-done | bytes 2621472 | tf_op jit(solution)/shard_map/all_to_all | solution.py:88
  123.7 0.0 copy-start.5
  123.7 3.1 %convolution_convert_fusion = bf16[32,512]{1,0:T(8,128)(2,1)S(1)} fusion(f32[32,2560]{1,0:T(8,128)S(1)} %reshape.343, bf16[2560,512]{1,0:T(8,128)(2,1)} %bitcast.7), kind=kOutput, calls=%fused_computation.5 | convolution fusion | flops 503332864 | bytes 2981888 | tf_op jit(solution)/shard_map/dot_general | solution.py:91
  126.8 0.0 copy-done.1
  126.8 0.3 convolution_add_fusion
  127.1 13.3 %all_to_all.26 = f32[2,32,1024]{2,1,0:T(8,128)S(1)} all-to-all(f32[2,32,1024]{2,1,0:T(8,128)S(1)} %broadcast_in_dim.20), channel_id=1, replica_groups=mesh['groups'=2,'rows'=64,'cols'=2] {'cols'}, dimensions={0} | all-to-all | bytes 524288 | tf_op jit(solution)/shard_map/all_to_all | solution.py:14
  140.4 0.0 copy-done.5
  140.5 0.1 multiply_reduce_fusion
  140.6 0.7 dynamic-slice_multiply_fusion
  (20 shorter events, 0.2 us)
Async XLA Ops:
  0.0 80.3 %copy-start = (bf16[512,1024]{1,0:T(8,128)(2,1)S(1)}, bf16[512,1024]{1,0:T(8,128)(2,1)}, u32[]{:S(2)}) copy-start(bf16[512,1024]{1,0:T(8,128)(2,1)} %param.11) | copy-start | bytes 3145732
  0.0 6.8 %copy-start.6 = (s32[3]{0:T(128)S(1)}, s32[3]{0:T(128)}, u32[]{:S(2)}) copy-start(s32[3]{0:T(128)} %constant.90) | copy-start | bytes 40
  0.0 6.9 %copy-start.9 = (s32[3]{0:T(128)S(1)}, s32[3]{0:T(128)}, u32[]{:S(2)}) copy-start(s32[3]{0:T(128)} %constant.93) | copy-start | bytes 40
  61.5 7.5 %copy-start.2 = (s32[32,50]{1,0:T(8,128)S(1)}, s32[32,50]{1,0:T(8,128)}, u32[]{:S(2)}) copy-start(s32[32,50]{1,0:T(8,128)} %param.9) | copy-start | bytes 19204
  61.6 8.0 %copy-start.4 = (f32[32,50]{1,0:T(8,128)S(1)}, f32[32,50]{1,0:T(8,128)}, u32[]{:S(2)}) copy-start(f32[32,50]{1,0:T(8,128)} %param.10) | copy-start | bytes 19204
  61.6 8.3 %copy-start.8 = (s32[2]{0:T(128)S(1)}, s32[2]{0:T(128)}, u32[]{:S(2)}) copy-start(s32[2]{0:T(128)} %constant.84) | copy-start | bytes 28
  61.6 8.4 %copy-start.7 = (s32[2]{0:T(128)S(1)}, s32[2]{0:T(128)}, u32[]{:S(2)}) copy-start(s32[2]{0:T(128)} %constant.87) | copy-start | bytes 28
  61.6 18.7 %copy-start.3 = (f32[32,512]{1,0:T(8,128)S(1)}, f32[32,512]{1,0:T(8,128)}, u32[]{:S(2)}) copy-start(f32[32,512]{1,0:T(8,128)} %param.8) | copy-start | bytes 196612
  61.6 62.1 %all-to-all-start.1 = ((bf16[64,40,512]{2,1,0:T(8,128)(2,1)}), bf16[64,40,512]{2,1,0:T(8,128)(2,1)}, u32[]{:S(2)}, u32[]{:S(2)}) async-start(bf16[64,40,512]{2,1,0:T(8,128)(2,1)} %select_convert_fusion), calls=%async_computation.1 | async-start | bytes 5242880 | tf_op jit(solution)/shard_map/all_to_all | solution.py:88
  70.1 56.7 %copy-start.1 = (bf16[512,1024]{1,0:T(8,128)(2,1)S(1)}, bf16[512,1024]{1,0:T(8,128)(2,1)}, u32[]{:S(2)}) copy-start(bf16[512,1024]{1,0:T(8,128)(2,1)} %param.12) | copy-start | bytes 3145732
  123.7 16.7 %copy-start.5 = (f32[1024]{0:T(1024)S(1)}, f32[1024]{0:T(1024)}, u32[]{:S(2)}) copy-start(f32[1024]{0:T(1024)} %param.13) | copy-start | bytes 12292
where the time goes:
time: 143 us; the launch traced here: 141 us
  blocking collectives  44.8 us (31%)
  waiting for transfers between devices  43.1 us (30%)
  local copies, waits for them, and re-layouts  22.5 us (16%)
  other arithmetic  19.5 us (14%)
  starting transfers between devices  7.36 us (5%)
  matrix products  3.64 us (3%)
    all_to_all x1, waiting for transfers between devices, body(): lax.all_to_all(found.astype(jnp.bfloat16), 'rows', split_axis=0, concat_a...  43.1 us
    all_to_all x1, blocking collectives, body(): lax.all_to_all(outgoing, 'rows', split_axis=0, concat_axis=0, tiled=True)  31.5 us
    all_to_all x1, blocking collectives, from_everyone(): lax.all_to_all(jnp.broadcast_to(array[None], (count, *array.shape)), axis...  13.3 us
    gather x1, local copies, waits for them, and re-layouts, body(): jnp.take(feature_table, lax.all_to_all(outgoing, 'rows', split_axis=0, co...  10.5 us
    unnamed x7, other arithmetic  10.5 us
    unnamed x24, local copies, waits for them, and re-layouts  9.02 us
    all_to_all x1, starting transfers between devices, body(): lax.all_to_all(found.astype(jnp.bfloat16), 'rows', split_axis=0, concat_a...  7.36 us
    another operation x4, other arithmetic  4.42 us
  transfers between devices with their start and end apart: 1, of which 1 were waited for; matrix products, arithmetic and copies ran while one was open for 8% of the time, Pallas kernels for 0%

commit v1 on v0

v1 whole, which is shorter than its diff:
```python
import functools
import math

import jax
import jax.numpy as jnp
from jax import lax
from jax.experimental import pallas as pl
from jax.experimental.pallas import tpu as pltpu
from jax.sharding import PartitionSpec as P

MESH = pl.DeviceIdType.MESH
NEIGH = 50
TGT = 16
CAP = 20
LANES = 128
F32 = jnp.float32
BF16 = jnp.bfloat16


def kernel(
    n,
    rows_dev,
    table_hbm,
    own_hbm,
    ids_hbm,
    imp_hbm,
    wself_hbm,
    wpool_hbm,
    bias_hbm,
    out_ref,
    tab,
    own_v,
    ids_v,
    imp_v,
    wself_v,
    wpool_v,
    bias_v,
    onehot,
    prefix,
    msg,
    got1,
    mid,
    got2,
    slots_v,
    slots_s,
    tgt_of,
    share_of,
    rows_g,
    self_part,
    rs_out,
    rs_in,
    fin,
    p2_in,
    ex_out,
    ex_in,
    in_sem,
    slot_sem,
    a1_send,
    a1_recv,
    a2_send,
    a2_recv,
    rs_send,
    rs_recv,
    p2_send,
    p2_recv,
    ex_sem,
):
    me = lax.axis_index("rows")
    col = lax.axis_index("cols")
    x = lax.rem(me, n)
    y = lax.div(me, n)
    owners = n * n
    half = n // 2
    width = own_v.shape[1]
    pieces = width // LANES
    tq = pieces // 2
    per_dev = own_v.shape[0]
    blocks = per_dev // TGT
    ring = lambda v: lax.rem(v + 2 * n, n)

    def along_x(k):
        return {"rows": y * n + ring(x + k)}

    def along_y(k):
        return {"rows": ring(y + k) * n + x}

    loads = [
        pltpu.make_async_copy(ids_hbm, ids_v, in_sem.at[0]),
        pltpu.make_async_copy(imp_hbm, imp_v, in_sem.at[1]),
        pltpu.make_async_copy(own_hbm, own_v, in_sem.at[2]),
        pltpu.make_async_copy(wself_hbm, wself_v, in_sem.at[3]),
        pltpu.make_async_copy(wpool_hbm, wpool_v, in_sem.at[4]),
        pltpu.make_async_copy(bias_hbm, bias_v, in_sem.at[5]),
    ]
    tab4 = tab.reshape(rows_dev // 8, pieces, 8, LANES)
    table_loads = [
        pltpu.make_async_copy(
            table_hbm.at[:, :, pl.ds(c * LANES, LANES)], tab4.at[:, c], in_sem.at[6 + c]
        )
        for c in range(pieces)
    ]
    for cp in loads[:2] + table_loads + loads[2:]:
        cp.start()

    barrier = pltpu.get_barrier_semaphore()
    for k in range(1, n):
        pl.semaphore_signal(barrier, inc=1, device_id=along_x(k), device_id_type=MESH)
        pl.semaphore_signal(barrier, inc=1, device_id=along_y(k), device_id_type=MESH)
    sibling = {"cols": 1 - col}
    pl.semaphore_signal(barrier, inc=1, device_id=sibling, device_id_type=MESH)

    loads[0].wait()
    loads[1].wait()
    lane = lax.broadcasted_iota(jnp.int32, (1, LANES), 1)
    owner_row = lax.broadcasted_iota(jnp.int32, (owners, LANES), 0)
    ids = ids_v[...]
    owner = ids >> int(math.log2(rows_dev))
    owner = jnp.where(ids < 0, -1, (owner & (n - 1)) * n + (owner >> int(math.log2(n))))
    for p in range(TGT):
        onehot[p * owners : (p + 1) * owners, :] = jnp.where(
            owner[p : p + 1] == owner_row, 1.0, 0.0
        ).astype(BF16)
    li = lax.broadcasted_iota(jnp.int32, (LANES, 2 * LANES), 0)
    lj = lax.broadcasted_iota(jnp.int32, (LANES, 2 * LANES), 1)
    hl = LANES // 2
    same = ((li // hl) == ((lj & (LANES - 1)) // hl)) & ((li < lj) | (lj >= LANES))
    prefix[...] = jnp.dot(
        onehot[...], jnp.where(same, 1.0, 0.0).astype(BF16), preferred_element_type=F32
    )
    imp = imp_v[...]
    left = jnp.sum(jnp.where(lane < hl, imp, 0.0), axis=1, keepdims=True)
    right = jnp.sum(jnp.where(lane >= hl, imp, 0.0), axis=1, keepdims=True)
    share = imp / jnp.where(lane < hl, left, right)
    local = ids & (rows_dev - 1)
    low = (local & 255).astype(F32)
    trow = lax.broadcasted_iota(jnp.int32, (TGT, LANES), 0)
    high = ((local >> 8) + trow * (rows_dev // 256)).astype(F32)
    share_hi = share.astype(BF16).astype(F32)
    share_lo = share - share_hi
    si = lax.broadcasted_iota(jnp.int32, (LANES, LANES), 0)
    sj = lax.broadcasted_iota(jnp.int32, (LANES, LANES), 1)
    slot_id = jnp.where(((si >> 5) & 1) == (sj // hl), si & 31, -1).astype(F32)
    base = jnp.zeros((owners, LANES), F32)
    acc = jnp.zeros((4 * owners, LANES), F32)
    for p in range(0, TGT, 2):
        lhs = []
        rhs = []
        for q in (p, p + 1):
            hot = onehot[q * owners : (q + 1) * owners, :].astype(F32)
            rank = jnp.sum(
                hot * (prefix[q * owners : (q + 1) * owners, :LANES] + base), axis=0, keepdims=True
            )
            base = base + prefix[q * owners : (q + 1) * owners, LANES:]
            rhs.append(jnp.where(slot_id == rank, 1.0, 0.0).astype(BF16))
            lhs.append(
                jnp.concatenate(
                    [hot * v[q : q + 1] for v in (low, high, share_hi, share_lo)], axis=0
                ).astype(BF16)
            )
        acc = acc + lax.dot_general(
            jnp.concatenate(lhs, axis=1),
            jnp.concatenate(rhs, axis=1),
            (((1,), (1,)), ((), ())),
            preferred_element_type=F32,
        )
    msg[0] = acc[:owners] + 256.0 * acc[owners : 2 * owners]
    msg[1] = acc[2 * owners : 3 * owners] + acc[3 * owners :]

    pad = jnp.zeros(((32 - CAP) * pieces, LANES), F32)

    def clear(i, carry):
        rows_g[pl.ds((i * 32 + CAP) * pieces, (32 - CAP) * pieces), :] = pad
        return carry

    lax.fori_loop(0, owners * blocks, clear, 0)

    pl.semaphore_wait(barrier, 2 * (n - 1) + 1)

    def hop1(k):
        to = ring(x + k)
        return pltpu.make_async_remote_copy(
            src_ref=msg.at[:, pl.ds(pl.multiple_of(to * n, n), n), :],
            dst_ref=got1.at[:, pl.ds(pl.multiple_of(x * n, n), n), :],
            send_sem=a1_send.at[k],
            recv_sem=a1_recv.at[k],
            device_id=along_x(k),
            device_id_type=MESH,
        )

    def hop2(k):
        return pltpu.make_async_remote_copy(
            src_ref=mid.at[ring(y + k)],
            dst_ref=got2.at[y],
            send_sem=a2_send.at[k],
            recv_sem=a2_recv.at[k],
            device_id=along_y(k),
            device_id_type=MESH,
        )

    order = sorted(range(1, n), key=lambda k: -min(k, n - k))
    for k in order:
        hop1(k).start()
    mine = pl.ds(pl.multiple_of(x * n, n), n)
    got1[:, mine, :] = msg[:, mine, :]

    loads[2].wait()
    loads[3].wait()
    self_part[...] = jnp.dot(own_v[...].astype(BF16), wself_v[...], preferred_element_type=F32)

    for k in order:
        hop1(k).wait_recv()
    for to in range(n):
        for plane in range(2):
            mid[to, plane * n : (plane + 1) * n, :] = got1[plane, pl.ds(to, n, stride=n), :]
    for k in order:
        hop2(k).start()
    got2[y] = mid[y]
    for cp in table_loads:
        cp.wait()
    for k in order:
        hop2(k).wait_recv()

    for s in range(n):
        packed = got2[s, :n, :].astype(jnp.int32)
        row = packed & (rows_dev - 1)
        slots_v[s * n : (s + 1) * n, :] = (row >> 3) * (8 * pieces) + (row & 7)
        tgt_of[s * n : (s + 1) * n, :] = (
            (packed >> int(math.log2(rows_dev))) + TGT * ((lane >> 5) & 1)
        ).astype(F32)
        share_of[s * n : (s + 1) * n, :] = got2[s, n:, :]
    to_scalar = pltpu.make_async_copy(slots_v, slots_s, slot_sem)
    to_scalar.start()
    to_scalar.wait()

    def gather(d, carry):
        for b in range(blocks):
            for s in range(CAP):
                start = slots_s[d, b * 32 + s]
                k = d * (32 * blocks) + b * 32 + s
                rows_g[pl.ds(k * pieces, pieces), :] = tab[pl.ds(start, pieces, stride=8), :]
        return carry

    lax.fori_loop(0, owners, gather, 0)

    group = 32 * blocks
    m = half * per_dev
    mi = lax.broadcasted_iota(jnp.int32, (m, LANES), 0).astype(F32)

    def partial(side, dest, sub):
        devs = [
            (sub * half + i) * n + dest if side == 0 else dest * n + sub * half + i
            for i in range(half)
        ]
        vals = jnp.concatenate(
            [
                jnp.concatenate(
                    [
                        rows_g[
                            pl.ds(d * (group * pieces) + side * tq + c, group, stride=pieces), :
                        ].astype(BF16)
                        for c in range(tq)
                    ],
                    axis=1,
                )
                for d in devs
            ],
            axis=0,
        )
        pick = []
        for j in range(0, half, 2):
            t = jnp.where(
                lane < hl,
                tgt_of[pl.ds(devs[j], 1), :] + float(j * per_dev),
                tgt_of[pl.ds(devs[j + 1], 1), :] + float((j + 1) * per_dev),
            )
            w = jnp.where(lane < hl, share_of[pl.ds(devs[j], 1), :], share_of[pl.ds(devs[j + 1], 1), :])
            pick.append(jnp.where(mi == t, w, 0.0).astype(BF16))
        return jnp.dot(jnp.concatenate(pick, axis=1), vals, preferred_element_type=F32)

    def hop(side, way, stage, sub):
        k = 1 if way == 0 else -1
        return pltpu.make_async_remote_copy(
            src_ref=rs_out.at[side, way, stage, sub],
            dst_ref=rs_in.at[side, way, stage, sub],
            send_sem=rs_send.at[side, way, stage, sub],
            recv_sem=rs_recv.at[side, way, stage, sub],
            device_id=along_x(k) if side == 0 else along_y(k),
            device_id_type=MESH,
        )

    def dest_of(side, way, stage):
        k = half - stage
        here = x if side == 0 else y
        return ring(here + k) if way == 0 else ring(here - k)

    for side in range(2):
        for way in range(2):
            rs_out[side, way, 0, way] = partial(side, dest_of(side, way, 0), way).astype(BF16)
            hop(side, way, 0, way).start()
    for side in range(2):
        for way in range(2):
            sub = 1 - way
            rs_out[side, way, 1, sub] = partial(side, dest_of(side, way, 1), sub).astype(BF16)
            hop(side, way, 1, sub).start()

    def stage_step(side, way, stage, sub):
        own = partial(side, dest_of(side, way, stage), sub)
        hop(side, way, stage - 1, sub).wait_recv()
        rs_out[side, way, stage, sub] = (
            own + rs_in[side, way, stage - 1, sub].astype(F32)
        ).astype(BF16)
        hop(side, way, stage, sub).start()

    for side in range(2):
        for way in range(2):
            stage_step(side, way, 1, way)

    def stages(stage, carry):
        for first in (1, 0):
            for side in range(2):
                for way in range(2):
                    stage_step(side, way, stage, way ^ first)
        return carry

    lax.fori_loop(2, half, stages, 0)

    def hop3(side, k):
        here = x if side == 1 else y
        return pltpu.make_async_remote_copy(
            src_ref=fin.at[side, ring(here + k)],
            dst_ref=p2_in.at[side, here],
            send_sem=p2_send.at[side, k],
            recv_sem=p2_recv.at[side, k],
            device_id=along_x(k) if side == 1 else along_y(k),
            device_id_type=MESH,
        )

    last = half - 1
    for side in range(2):
        for sub in range(2):
            total = partial(side, x if side == 0 else y, sub)
            for way in range(2):
                hop(side, way, last, sub).wait_recv()
                total = total + rs_in[side, way, last, sub].astype(F32)
            for i in range(half):
                fin[side, sub * half + i] = total[i * per_dev : (i + 1) * per_dev].astype(BF16)
        for k in order:
            hop3(side, k).start()

    sums = []
    for side in range(2):
        here = x if side == 1 else y
        total = fin[side, here].astype(F32)
        for k in order:
            hop3(side, k).wait_recv()
            total = total + p2_in[side, ring(here - k)].astype(F32)
        sums.append(total)
    pooled = jnp.concatenate(sums, axis=1).astype(BF16)
    loads[4].wait()
    loads[5].wait()
    ex_out[...] = self_part[...] + jnp.dot(pooled, wpool_v[...], preferred_element_type=F32)
    swap = pltpu.make_async_remote_copy(
        src_ref=ex_out,
        dst_ref=ex_in,
        send_sem=ex_sem.at[0],
        recv_sem=ex_sem.at[1],
        device_id=sibling,
        device_id_type=MESH,
    )
    swap.start()
    swap.wait_recv()
    hidden = jnp.maximum(ex_out[...] + ex_in[...] + bias_v[...], 0.0)
    scale = lax.rsqrt(jnp.sum(hidden * hidden, axis=1, keepdims=True) / hidden.shape[1] + 1e-6)
    columns = pl.ds(pl.multiple_of(col * width, width), width)
    mine_hidden = jnp.maximum(ex_out[:, columns] + ex_in[:, columns] + bias_v[:, columns], 0.0)
    out_ref[...] = mine_hidden * scale

    swap.wait_send()
    for k in range(1, n):
        hop1(k).wait_send()
        hop2(k).wait_send()
        for side in range(2):
            hop3(side, k).wait_send()
    for side in range(2):
        for way in range(2):
            hop(side, way, 0, way).wait_send()
            for stage in range(1, half):
                for sub in range(2):
                    hop(side, way, stage, sub).wait_send()


def body(feature_table, own_features, neighbor_ids, importance, w_self, w_pool, bias):
    rows_dev, width = feature_table.shape
    per_dev = own_features.shape[0]
    blocks = per_dev // TGT
    full = w_self.shape[1]
    n = math.isqrt(lax.axis_size("rows"))
    owners = n * n
    half = n // 2
    pieces = width // LANES
    slots = 32 * blocks
    lay = lambda a, fill: jnp.concatenate(
        [
            jnp.pad(part, ((0, 0), (0, LANES // 2 - NEIGH)), constant_values=fill)
            for part in (a[:TGT], a[TGT:])
        ],
        axis=1,
    )
    anyspace = pl.BlockSpec(memory_space=pl.ANY)
    dma = pltpu.SemaphoreType.DMA
    sub_rows = half * per_dev
    return pl.pallas_call(
        functools.partial(kernel, n, rows_dev),
        out_shape=jax.ShapeDtypeStruct((per_dev, width), F32),
        in_specs=[anyspace] * 7,
        out_specs=pl.BlockSpec(memory_space=pltpu.VMEM),
        scratch_shapes=[
            pltpu.VMEM((rows_dev * pieces, LANES), F32),
            pltpu.VMEM((per_dev, width), F32),
            pltpu.VMEM((TGT, LANES), jnp.int32),
            pltpu.VMEM((TGT, LANES), F32),
            pltpu.VMEM((width, full), BF16),
            pltpu.VMEM((width, full), BF16),
            pltpu.VMEM((1, full), F32),
            pltpu.VMEM((TGT * owners, LANES), BF16),
            pltpu.VMEM((TGT * owners, 2 * LANES), F32),
            pltpu.VMEM((2, owners, LANES), F32),
            pltpu.VMEM((2, owners, LANES), F32),
            pltpu.VMEM((n, 2 * n, LANES), F32),
            pltpu.VMEM((n, 2 * n, LANES), F32),
            pltpu.VMEM((owners, LANES), jnp.int32),
            pltpu.SMEM((owners, LANES), jnp.int32),
            pltpu.VMEM((owners, LANES), F32),
            pltpu.VMEM((owners, LANES), F32),
            pltpu.VMEM((owners * slots * pieces, LANES), F32),
            pltpu.VMEM((per_dev, full), F32),
            pltpu.VMEM((2, 2, half, 2, sub_rows, width // 2), BF16),
            pltpu.VMEM((2, 2, half, 2, sub_rows, width // 2), BF16),
            pltpu.VMEM((2, n, per_dev, width // 2), BF16),
            pltpu.VMEM((2, n, per_dev, width // 2), BF16),
            pltpu.VMEM((per_dev, full), F32),
            pltpu.VMEM((per_dev, full), F32),
            dma((6 + pieces,)),
            dma,
            dma((n,)),
            dma((n,)),
            dma((n,)),
            dma((n,)),
            dma((2, 2, half, 2)),
            dma((2, 2, half, 2)),
            dma((2, n)),
            dma((2, n)),
            dma((2,)),
        ],
        compiler_params=pltpu.CompilerParams(
            collective_id=0, has_side_effects=True, vmem_limit_bytes=48 * 1024 * 1024
        ),
    )(
        feature_table.reshape(rows_dev // 8, 8, width),
        own_features,
        lay(neighbor_ids, -1),
        lay(importance, 0),
        w_self,
        w_pool,
        bias.reshape(1, full),
    )


def solution(mesh):
    placed = (
        P(("groups", "rows"), "cols"),
        P(("groups", "rows"), "cols"),
        P(("groups", "rows"), None),
        P(("groups", "rows"), None),
        P("cols", None),
        P("cols", None),
        P(),
    )
    return jax.shard_map(
        body, mesh=mesh, in_specs=placed, out_specs=P(("groups", "rows"), "cols"), check_vma=False
    )
```

time: 143 us -> 67.9 us (0.47)
  Pallas kernels: 0 us -> 61.4 us
  blocking collectives: 44.8 us -> 0 us
  waiting for transfers between devices: 43.1 us -> 0 us
  other arithmetic: 19.5 us -> 0.15 us
  local copies, waits for them, and re-layouts: 22.5 us -> 6.04 us
  starting transfers between devices: 7.36 us -> 0 us
  matrix products: 3.64 us -> 0 us
    pallas_call x0 -> x1, Pallas kernels: none -> 61.4 us  [body(): pl.pallas_call(functools.partial(kernel, n, rows_dev), out_shape=jax.Shap...]
    all_to_all x2 -> x0, blocking collectives: 44.8 us -> none  [the longest x1 31.5 us: body(): lax.all_to_all(outgoing, 'rows', split_axis=0, concat_axis=0, tiled=True)]
    all_to_all x1 -> x0, waiting for transfers between devices: 43.1 us -> none  [body(): lax.all_to_all(found.astype(jnp.bfloat16), 'rows', split_axis=0, concat_a...]
    gather x1 -> x0, local copies, waits for them, and re-layouts: 10.5 us -> none  [body(): jnp.take(feature_table, lax.all_to_all(outgoing, 'rows', split_axis=0, co...]
    unnamed x7 -> x0, other arithmetic: 10.5 us -> none
    all_to_all x1 -> x0, starting transfers between devices: 7.36 us -> none  [body(): lax.all_to_all(found.astype(jnp.bfloat16), 'rows', split_axis=0, concat_a...]
    another operation x4 -> x0, other arithmetic: 4.42 us -> none
    unnamed x24 -> x9, local copies, waits for them, and re-layouts: 9.02 us -> 4.61 us
  transfers between devices with their start and end apart: 1 -> 0, of which waited for: 1 -> 0; matrix products, arithmetic and copies ran while one was open for 8% -> 0% of each run, Pallas kernels for 0% -> 0%
where the time goes in v1:
time: 67.9 us; the launch traced here: 67.6 us
  Pallas kernels  61.4 us (90%)
  local copies, waits for them, and re-layouts  6.04 us (9%)
    pallas_call x1, Pallas kernels, body(): pl.pallas_call(functools.partial(kernel, n, rows_dev), out_shape=jax.Shap...  61.4 us
    unnamed x9, local copies, waits for them, and re-layouts  4.61 us
    slice x2, local copies, waits for them, and re-layouts, body(): a[:TGT]  1.43 us

profile of v1, /device:TPU:513, one launch (start us, length us, event | category | flops | bytes accessed | tf_op | source)
XLA Modules:
  0.0 67.6 jit_solution(553193049877437153)
XLA Ops:
  0.0 0.7 %fusion.1 = (s32[16,50]{1,0:T(8,128)S(1)}, s32[16,50]{1,0:T(8,128)S(1)}) fusion(s32[32,50]{1,0:T(8,128)} %param.9), kind=kLoop, calls=%fused_computation.5 | loop fusion | bytes 12800 | tf_op jit(solution)/shard_map/slice | solution.py:405
  0.7 0.1 select_add_fusion.ids_hbm
  0.8 0.7 %fusion = (f32[16,50]{1,0:T(8,128)S(1)}, f32[16,50]{1,0:T(8,128)S(1)}) fusion(f32[32,50]{1,0:T(8,128)} %param.10), kind=kLoop, calls=%fused_computation.4 | loop fusion | bytes 12800 | tf_op jit(solution)/shard_map/slice | solution.py:405
  1.5 0.1 select_maximum_fusion.imp_hbm
  1.6 0.0 copy-start
  1.6 1.2 %copy-done = bf16[512,1024]{1,0:T(8,128)(2,1)S(1)} copy-done((bf16[512,1024]{1,0:T(8,128)(2,1)S(1)}, bf16[512,1024]{1,0:T(8,128)(2,1)}, u32[]{:S(2)}) %copy-start) | copy-done | bytes 1048600
  2.8 0.0 copy-start.1
  2.8 1.2 %copy-done.1 = bf16[512,1024]{1,0:T(8,128)(2,1)S(1)} copy-done((bf16[512,1024]{1,0:T(8,128)(2,1)S(1)}, bf16[512,1024]{1,0:T(8,128)(2,1)}, u32[]{:S(2)}) %copy-start.1) | copy-done | bytes 1048600
  4.0 0.0 copy-start.2
  4.0 0.8 %copy-done.2 = f32[32,512]{1,0:T(8,128)S(1)} copy-done((f32[32,512]{1,0:T(8,128)S(1)}, f32[32,512]{1,0:T(8,128)}, u32[]{:S(2)}) %copy-start.2) | copy-done | bytes 65560
  4.9 0.0 copy-start.3
  4.9 0.7 %copy-done.3 = f32[1024]{0:T(1024)S(1)} copy-done((f32[1024]{0:T(1024)S(1)}, f32[1024]{0:T(1024)}, u32[]{:S(2)}) %copy-start.3) | copy-done | bytes 4120
  5.6 61.4 %shard_map.73 = f32[32,512]{1,0:T(8,128)S(1)} custom-call(f32[256,8,512]{2,1,0:T(8,128)} %bitcast.3, f32[32,512]{1,0:T(8,128)S(1)} %copy-done.2, s32[16,128]{1,0:T(8,128)S(1)} %select_add_fusion.ids_hbm, f32[16,128]{1,0:T(8,128)S(1)} %select_maximum_fusion.imp_hbm, bf16[512,1024]{1,0:T(8,128)(2,1)S(1)} %copy-done, bf16[512,1024]{1,0:T(8,128)(2,1)S(1)} %copy-done.1, ...), custom_call_target="tpu_custom_call" | custom-call | tf_op jit(solution)/shard_map/pallas_call | solution.py:412
  66.9 0.6 copy.9
Async XLA Ops:
  1.6 1.2 %copy-start = (bf16[512,1024]{1,0:T(8,128)(2,1)S(1)}, bf16[512,1024]{1,0:T(8,128)(2,1)}, u32[]{:S(2)}) copy-start(bf16[512,1024]{1,0:T(8,128)(2,1)} %wself_hbm.1) | copy-start | bytes 3145732
  2.8 1.2 %copy-start.1 = (bf16[512,1024]{1,0:T(8,128)(2,1)S(1)}, bf16[512,1024]{1,0:T(8,128)(2,1)}, u32[]{:S(2)}) copy-start(bf16[512,1024]{1,0:T(8,128)(2,1)} %wpool_hbm.1) | copy-start | bytes 3145732
  4.0 0.8 %copy-start.2 = (f32[32,512]{1,0:T(8,128)S(1)}, f32[32,512]{1,0:T(8,128)}, u32[]{:S(2)}) copy-start(f32[32,512]{1,0:T(8,128)} %own_hbm.1) | copy-start | bytes 196612
  4.9 0.7 %copy-start.3 = (f32[1024]{0:T(1024)S(1)}, f32[1024]{0:T(1024)}, u32[]{:S(2)}) copy-start(f32[1024]{0:T(1024)} %param.13) | copy-start | bytes 12292

commit v2 on v1

--- a/solution.py
+++ b/solution.py
@@ -47,6 +47,7 @@
     share_of,
     rows_g,
     self_part,
+    own_sum,
     rs_out,
     rs_in,
     fin,
@@ -113,21 +114,27 @@
     loads[1].wait()
     lane = lax.broadcasted_iota(jnp.int32, (1, LANES), 1)
     owner_row = lax.broadcasted_iota(jnp.int32, (owners, LANES), 0)
-    ids = ids_v[...]
+    hl = LANES // 2
+
+    def lay(a):
+        room = jnp.zeros((TGT, hl - NEIGH), a.dtype)
+        return jnp.concatenate([a[:TGT], room, a[TGT:], room], axis=1)
+
+    real = (lane & (hl - 1)) < NEIGH
+    ids = lay(ids_v[...])
     owner = ids >> int(math.log2(rows_dev))
-    owner = jnp.where(ids < 0, -1, (owner & (n - 1)) * n + (owner >> int(math.log2(n))))
+    owner = jnp.where(real, (owner & (n - 1)) * n + (owner >> int(math.log2(n))), -1)
     for p in range(TGT):
         onehot[p * owners : (p + 1) * owners, :] = jnp.where(
             owner[p : p + 1] == owner_row, 1.0, 0.0
         ).astype(BF16)
     li = lax.broadcasted_iota(jnp.int32, (LANES, 2 * LANES), 0)
     lj = lax.broadcasted_iota(jnp.int32, (LANES, 2 * LANES), 1)
-    hl = LANES // 2
     same = ((li // hl) == ((lj & (LANES - 1)) // hl)) & ((li < lj) | (lj >= LANES))
     prefix[...] = jnp.dot(
         onehot[...], jnp.where(same, 1.0, 0.0).astype(BF16), preferred_element_type=F32
     )
-    imp = imp_v[...]
+    imp = lay(imp_v[...])
     left = jnp.sum(jnp.where(lane < hl, imp, 0.0), axis=1, keepdims=True)
     right = jnp.sum(jnp.where(lane >= hl, imp, 0.0), axis=1, keepdims=True)
     share = imp / jnp.where(lane < hl, left, right)
@@ -163,24 +170,19 @@
             (((1,), (1,)), ((), ())),
             preferred_element_type=F32,
         )
-    msg[0] = acc[:owners] + 256.0 * acc[owners : 2 * owners]
-    msg[1] = acc[2 * owners : 3 * owners] + acc[3 * owners :]
-
-    pad = jnp.zeros(((32 - CAP) * pieces, LANES), F32)
-
-    def clear(i, carry):
-        rows_g[pl.ds((i * 32 + CAP) * pieces, (32 - CAP) * pieces), :] = pad
-        return carry
-
-    lax.fori_loop(0, owners * blocks, clear, 0)
+    msg[...] = jnp.where(
+        lane < hl,
+        acc[:owners] + 256.0 * acc[owners : 2 * owners],
+        acc[2 * owners : 3 * owners] + acc[3 * owners :],
+    )
 
     pl.semaphore_wait(barrier, 2 * (n - 1) + 1)
 
     def hop1(k):
         to = ring(x + k)
         return pltpu.make_async_remote_copy(
-            src_ref=msg.at[:, pl.ds(pl.multiple_of(to * n, n), n), :],
-            dst_ref=got1.at[:, pl.ds(pl.multiple_of(x * n, n), n), :],
+            src_ref=msg.at[pl.ds(pl.multiple_of(to * n, n), n), :],
+            dst_ref=got1.at[pl.ds(pl.multiple_of(x * n, n), n), :],
             send_sem=a1_send.at[k],
             recv_sem=a1_recv.at[k],
             device_id=along_x(k),
@@ -201,46 +203,72 @@
     for k in order:
         hop1(k).start()
     mine = pl.ds(pl.multiple_of(x * n, n), n)
-    got1[:, mine, :] = msg[:, mine, :]
+    got1[mine, :] = msg[mine, :]
+
+    pad = jnp.zeros(((32 - CAP) * pieces, LANES), F32)
+
+    def clear(i, carry):
+        rows_g[pl.ds((i * 32 + CAP) * pieces, (32 - CAP) * pieces), :] = pad
+        return carry
+
+    lax.fori_loop(0, owners * blocks, clear, 0)
 
     loads[2].wait()
     loads[3].wait()
     self_part[...] = jnp.dot(own_v[...].astype(BF16), wself_v[...], preferred_element_type=F32)
 
-    for k in order:
+    near = order[::-1]
+    for k in near:
         hop1(k).wait_recv()
     for to in range(n):
-        for plane in range(2):
-            mid[to, plane * n : (plane + 1) * n, :] = got1[plane, pl.ds(to, n, stride=n), :]
+        mid[to] = got1[pl.ds(to, n, stride=n), :]
     for k in order:
         hop2(k).start()
     got2[y] = mid[y]
     for cp in table_loads:
         cp.wait()
-    for k in order:
-        hop2(k).wait_recv()
-
-    for s in range(n):
-        packed = got2[s, :n, :].astype(jnp.int32)
+
+    def to_scalar(at):
+        rows = pl.ds(pl.multiple_of(at * n, n), n)
+        return pltpu.make_async_copy(
+            slots_v.at[rows, :], slots_s.at[rows, :], slot_sem.at[at]
+        )
+
+    def unpack(at):
+        rows = pl.ds(pl.multiple_of(at * n, n), n)
+        got = got2[at]
+        turned = pltpu.roll(got, hl, axis=1)
+        packed = jnp.where(lane < hl, got, turned).astype(jnp.int32)
         row = packed & (rows_dev - 1)
-        slots_v[s * n : (s + 1) * n, :] = (row >> 3) * (8 * pieces) + (row & 7)
-        tgt_of[s * n : (s + 1) * n, :] = (
+        slots_v[rows, :] = (row >> 3) * (8 * pieces) + (row & 7)
+        tgt_of[rows, :] = (
             (packed >> int(math.log2(rows_dev))) + TGT * ((lane >> 5) & 1)
         ).astype(F32)
-        share_of[s * n : (s + 1) * n, :] = got2[s, n:, :]
-    to_scalar = pltpu.make_async_copy(slots_v, slots_s, slot_sem)
-    to_scalar.start()
-    to_scalar.wait()
-
-    def gather(d, carry):
-        for b in range(blocks):
-            for s in range(CAP):
-                start = slots_s[d, b * 32 + s]
-                k = d * (32 * blocks) + b * 32 + s
-                rows_g[pl.ds(k * pieces, pieces), :] = tab[pl.ds(start, pieces, stride=8), :]
-        return carry
-
-    lax.fori_loop(0, owners, gather, 0)
+        share_of[rows, :] = jnp.where(lane < hl, turned, got)
+        to_scalar(at).start()
+
+    def gather(at):
+        to_scalar(at).wait()
+
+        def one(i, carry):
+            d = at * n + i
+            for b in range(blocks):
+                for s in range(CAP):
+                    start = slots_s[d, b * 32 + s]
+                    k = d * (32 * blocks) + b * 32 + s
+                    rows_g[pl.ds(k * pieces, pieces), :] = tab[pl.ds(start, pieces, stride=8), :]
+            return carry
+
+        lax.fori_loop(0, n, one, 0)
+
+    unpack(y)
+    before = y
+    for k in near:
+        hop2(k).wait_recv()
+        unpack(ring(y - k))
+        gather(before)
+        before = ring(y - k)
+    gather(before)
 
     group = 32 * blocks
     m = half * per_dev
@@ -277,13 +305,14 @@
             pick.append(jnp.where(mi == t, w, 0.0).astype(BF16))
         return jnp.dot(jnp.concatenate(pick, axis=1), vals, preferred_element_type=F32)
 
-    def hop(side, way, stage, sub):
+    def hop(side, way, stage, sub, part):
         k = 1 if way == 0 else -1
+        at = (side, way, stage, sub, part)
         return pltpu.make_async_remote_copy(
-            src_ref=rs_out.at[side, way, stage, sub],
-            dst_ref=rs_in.at[side, way, stage, sub],
-            send_sem=rs_send.at[side, way, stage, sub],
-            recv_sem=rs_recv.at[side, way, stage, sub],
+            src_ref=rs_out.at[at],
+            dst_ref=rs_in.at[at],
+            send_sem=rs_send.at[at],
+            recv_sem=rs_recv.at[at],
             device_id=along_x(k) if side == 0 else along_y(k),
             device_id_type=MESH,
         )
@@ -293,66 +322,92 @@
         here = x if side == 0 else y
         return ring(here + k) if way == 0 else ring(here - k)
 
-    for side in range(2):
-        for way in range(2):
-            rs_out[side, way, 0, way] = partial(side, dest_of(side, way, 0), way).astype(BF16)
-            hop(side, way, 0, way).start()
-    for side in range(2):
-        for way in range(2):
-            sub = 1 - way
-            rs_out[side, way, 1, sub] = partial(side, dest_of(side, way, 1), sub).astype(BF16)
-            hop(side, way, 1, sub).start()
-
-    def stage_step(side, way, stage, sub):
+    lanes4 = [(side, way) for side in range(2) for way in range(2)]
+    pm = m // 2
+
+    def send_first(side, way, stage, sub):
         own = partial(side, dest_of(side, way, stage), sub)
-        hop(side, way, stage - 1, sub).wait_recv()
-        rs_out[side, way, stage, sub] = (
-            own + rs_in[side, way, stage - 1, sub].astype(F32)
+        for part in range(2):
+            rs_out[side, way, stage, sub, part] = own[part * pm : (part + 1) * pm].astype(BF16)
+            hop(side, way, stage, sub, part).start()
+
+    def ahead(side, way, stage, sub):
+        own_sum[side, way, sub] = partial(side, dest_of(side, way, stage), sub)
+
+    def pass_on(side, way, stage, sub, part):
+        hop(side, way, stage - 1, sub, part).wait_recv()
+        rs_out[side, way, stage, sub, part] = (
+            own_sum[side, way, sub, pl.ds(part * pm, pm)]
+            + rs_in[side, way, stage - 1, sub, part].astype(F32)
         ).astype(BF16)
-        hop(side, way, stage, sub).start()
-
-    for side in range(2):
-        for way in range(2):
-            stage_step(side, way, 1, way)
-
-    def stages(stage, carry):
-        for first in (1, 0):
-            for side in range(2):
-                for way in range(2):
-                    stage_step(side, way, stage, way ^ first)
-        return carry
-
-    lax.fori_loop(2, half, stages, 0)
-
-    def hop3(side, k):
+        hop(side, way, stage, sub, part).start()
+
+    for side, way in lanes4:
+        send_first(side, way, 0, way)
+    for side, way in lanes4:
+        send_first(side, way, 1, 1 - way)
+    last = half - 1
+    for stage in range(1, half):
+        for side, way in lanes4:
+            ahead(side, way, stage, way)
+        for part in range(2):
+            for side, way in lanes4:
+                pass_on(side, way, stage, way, part)
+        if stage < last:
+            for side, way in lanes4:
+                ahead(side, way, stage + 1, 1 - way)
+            for part in range(2):
+                for side, way in lanes4:
+                    pass_on(side, way, stage + 1, 1 - way, part)
+
+    def hop3(side, to):
         here = x if side == 1 else y
         return pltpu.make_async_remote_copy(
-            src_ref=fin.at[side, ring(here + k)],
+            src_ref=fin.at[side, to],
             dst_ref=p2_in.at[side, here],
-            send_sem=p2_send.at[side, k],
-            recv_sem=p2_recv.at[side, k],
-            device_id=along_x(k) if side == 1 else along_y(k),
+            send_sem=p2_send.at[side, to],
+            recv_sem=p2_recv.at[side, here],
+            device_id={"rows": y * n + to} if side == 1 else {"rows": to * n + x},
             device_id_type=MESH,
         )
 
-    last = half - 1
+    def hop3_from(side, k):
+        here = x if side == 1 else y
+        there = ring(here - k)
+        return pltpu.make_async_remote_copy(
+            src_ref=fin.at[side, there],
+            dst_ref=p2_in.at[side, there],
+            send_sem=p2_send.at[side, there],
+            recv_sem=p2_recv.at[side, there],
+            device_id=along_x(-k) if side == 1 else along_y(-k),
+            device_id_type=MESH,
+        )
+
     for side in range(2):
         for sub in range(2):
-            total = partial(side, x if side == 0 else y, sub)
-            for way in range(2):
-                hop(side, way, last, sub).wait_recv()
-                total = total + rs_in[side, way, last, sub].astype(F32)
-            for i in range(half):
-                fin[side, sub * half + i] = total[i * per_dev : (i + 1) * per_dev].astype(BF16)
-        for k in order:
-            hop3(side, k).start()
+            own_sum[side, 0, sub] = partial(side, x if side == 0 else y, sub)
+    per_part = half // 2
+    for part in range(2):
+        for side in range(2):
+            for sub in range(2):
+                total = own_sum[side, 0, sub, pl.ds(part * pm, pm)]
+                for way in (1 - sub, sub):
+                    hop(side, way, last, sub, part).wait_recv()
+                    total = total + rs_in[side, way, last, sub, part].astype(F32)
+                for i in range(per_part):
+                    to = sub * half + part * per_part + i
+                    fin[side, to] = total[i * per_dev : (i + 1) * per_dev].astype(BF16)
+
+                    @pl.when(to != (x if side == 1 else y))
+                    def _():
+                        hop3(side, to).start()
 
     sums = []
     for side in range(2):
         here = x if side == 1 else y
         total = fin[side, here].astype(F32)
-        for k in order:
-            hop3(side, k).wait_recv()
+        for k in near:
+            hop3_from(side, k).wait_recv()
             total = total + p2_in[side, ring(here - k)].astype(F32)
         sums.append(total)
     pooled = jnp.concatenate(sums, axis=1).astype(BF16)
@@ -368,6 +423,17 @@
         device_id_type=MESH,
     )
     swap.start()
+    for k in range(1, n):
+        hop1(k).wait_send()
+        hop2(k).wait_send()
+        for side in range(2):
+            hop3_from(side, k).wait_send()
+    for side, way in lanes4:
+        for part in range(2):
+            hop(side, way, 0, way, part).wait_send()
+            for stage in range(1, half):
+                for sub in range(2):
+                    hop(side, way, stage, sub, part).wait_send()
     swap.wait_recv()
     hidden = jnp.maximum(ex_out[...] + ex_in[...] + bias_v[...], 0.0)
     scale = lax.rsqrt(jnp.sum(hidden * hidden, axis=1, keepdims=True) / hidden.shape[1] + 1e-6)
@@ -376,17 +442,6 @@
     out_ref[...] = mine_hidden * scale
 
     swap.wait_send()
-    for k in range(1, n):
-        hop1(k).wait_send()
-        hop2(k).wait_send()
-        for side in range(2):
-            hop3(side, k).wait_send()
-    for side in range(2):
-        for way in range(2):
-            hop(side, way, 0, way).wait_send()
-            for stage in range(1, half):
-                for sub in range(2):
-                    hop(side, way, stage, sub).wait_send()
 
 
 def body(feature_table, own_features, neighbor_ids, importance, w_self, w_pool, bias):
@@ -399,67 +454,61 @@
     half = n // 2
     pieces = width // LANES
     slots = 32 * blocks
-    lay = lambda a, fill: jnp.concatenate(
-        [
-            jnp.pad(part, ((0, 0), (0, LANES // 2 - NEIGH)), constant_values=fill)
-            for part in (a[:TGT], a[TGT:])
-        ],
-        axis=1,
-    )
-    anyspace = pl.BlockSpec(memory_space=pl.ANY)
+    in_hbm = pl.BlockSpec(memory_space=pltpu.HBM)
     dma = pltpu.SemaphoreType.DMA
     sub_rows = half * per_dev
     return pl.pallas_call(
         functools.partial(kernel, n, rows_dev),
         out_shape=jax.ShapeDtypeStruct((per_dev, width), F32),
-        in_specs=[anyspace] * 7,
+        in_specs=[in_hbm] * 7,
         out_specs=pl.BlockSpec(memory_space=pltpu.VMEM),
         scratch_shapes=[
             pltpu.VMEM((rows_dev * pieces, LANES), F32),
             pltpu.VMEM((per_dev, width), F32),
-            pltpu.VMEM((TGT, LANES), jnp.int32),
-            pltpu.VMEM((TGT, LANES), F32),
+            pltpu.VMEM((per_dev, NEIGH), jnp.int32),
+            pltpu.VMEM((per_dev, NEIGH), F32),
             pltpu.VMEM((width, full), BF16),
             pltpu.VMEM((width, full), BF16),
             pltpu.VMEM((1, full), F32),
             pltpu.VMEM((TGT * owners, LANES), BF16),
             pltpu.VMEM((TGT * owners, 2 * LANES), F32),
-            pltpu.VMEM((2, owners, LANES), F32),
-            pltpu.VMEM((2, owners, LANES), F32),
-            pltpu.VMEM((n, 2 * n, LANES), F32),
-            pltpu.VMEM((n, 2 * n, LANES), F32),
+            pltpu.VMEM((owners, LANES), F32),
+            pltpu.VMEM((owners, LANES), F32),
+            pltpu.VMEM((n, n, LANES), F32),
+            pltpu.VMEM((n, n, LANES), F32),
             pltpu.VMEM((owners, LANES), jnp.int32),
             pltpu.SMEM((owners, LANES), jnp.int32),
             pltpu.VMEM((owners, LANES), F32),
             pltpu.VMEM((owners, LANES), F32),
             pltpu.VMEM((owners * slots * pieces, LANES), F32),
             pltpu.VMEM((per_dev, full), F32),
-            pltpu.VMEM((2, 2, half, 2, sub_rows, width // 2), BF16),
-            pltpu.VMEM((2, 2, half, 2, sub_rows, width // 2), BF16),
+            pltpu.VMEM((2, 2, 2, sub_rows, width // 2), F32),
+            pltpu.VMEM((2, 2, half, 2, 2, sub_rows // 2, width // 2), BF16),
+            pltpu.VMEM((2, 2, half, 2, 2, sub_rows // 2, width // 2), BF16),
             pltpu.VMEM((2, n, per_dev, width // 2), BF16),
             pltpu.VMEM((2, n, per_dev, width // 2), BF16),
             pltpu.VMEM((per_dev, full), F32),
             pltpu.VMEM((per_dev, full), F32),
             dma((6 + pieces,)),
-            dma,
             dma((n,)),
             dma((n,)),
             dma((n,)),
             dma((n,)),
-            dma((2, 2, half, 2)),
-            dma((2, 2, half, 2)),
+            dma((n,)),
+            dma((2, 2, half, 2, 2)),
+            dma((2, 2, half, 2, 2)),
             dma((2, n)),
             dma((2, n)),
             dma((2,)),
         ],
         compiler_params=pltpu.CompilerParams(
-            collective_id=0, has_side_effects=True, vmem_limit_bytes=48 * 1024 * 1024
+            collective_id=0, has_side_effects=True, vmem_limit_bytes=67043328
         ),
     )(
         feature_table.reshape(rows_dev // 8, 8, width),
         own_features,
-        lay(neighbor_ids, -1),
-        lay(importance, 0),
+        neighbor_ids,
+        importance,
         w_self,
         w_pool,
         bias.reshape(1, full),

time: 67.9 us -> 59.4 us (0.87)
  local copies, waits for them, and re-layouts: 6.04 us -> 1.47 us
  Pallas kernels: 61.4 us -> 57.8 us
    pallas_call x1, Pallas kernels: 61.4 us -> 57.8 us  [body(): pl.pallas_call(functools.partial(kernel, n, rows_dev), out_shape=jax.Shap...]
    unnamed x9 -> x1, local copies, waits for them, and re-layouts: 4.61 us -> 1.47 us
    slice x2 -> x0, local copies, waits for them, and re-layouts: 1.43 us -> none  [body(): a[:TGT]]
where the time goes in v2:
time: 59.4 us; the launch traced here: 59.2 us
  Pallas kernels  57.8 us (97%)
  local copies, waits for them, and re-layouts  1.47 us (2%)
    pallas_call x1, Pallas kernels, body(): pl.pallas_call(functools.partial(kernel, n, rows_dev), out_shape=jax.Shap...  57.8 us
    unnamed x1, local copies, waits for them, and re-layouts  1.47 us

profile of v2, /device:TPU:513, one launch (start us, length us, event | category | flops | bytes accessed | tf_op | source)
XLA Modules:
  0.0 59.2 jit_solution(1795702523354384905)
XLA Ops:
  0.0 57.8 %shard_map.73 = f32[32,512]{1,0:T(8,128)} custom-call(f32[256,8,512]{2,1,0:T(8,128)} %bitcast.2, f32[32,512]{1,0:T(8,128)} %own_hbm.1, s32[32,50]{1,0:T(8,128)} %ids_hbm.1, f32[32,50]{1,0:T(8,128)} %imp_hbm.1, bf16[512,1024]{1,0:T(8,128)(2,1)} %wself_hbm.1, bf16[512,1024]{1,0:T(8,128)(2,1)} %wpool_hbm.1, f32[1,1024]{1,0:T(1,128)} %bitcast.3), custom_call_target="tpu_custom_call" | custom-call | tf_op jit(solution)/shard_map/pallas_call | solution.py:460
  57.8 1.5 %copy.9 = f32[32,512]{1,0:T(8,128)} copy(f32[32,512]{1,0:T(8,128)} %shard_map.73) | data formatting | bytes 131072
